TPU v7x, 32 devices: a whole 2x2x4 slice. The times are simulated.
32 devices in a mesh: dp: 4 (over x, core), mp: 8 (over z, y).
Axes of the slice: x: 2, y: 2, z: 4, core: 2. Of those that a mesh axis runs over, the one named last changes fastest.
Arguments:
- tokens: bfloat16 [1280, 1792], P(('dp', 'mp')), may hold values from -6 to 6
- norm_gain: float32 [1792], replicated, may hold values from 0.5 to 1.5
- norm_bias: float32 [1792], replicated, may hold values from -3 to 3
- w_in: bfloat16 [1792, 15360], P('dp', 'mp'), may hold values from -0.125 to 0.125
- b_in: float32 [15360], P('mp'), may hold values from -3 to 3
- w_out: bfloat16 [15360, 1792], P('mp', 'dp'), may hold values from -0.046875 to 0.046875
- b_out: float32 [1792], replicated, may hold values from -3 to 3
Outputs:
- result: bfloat16 [1280, 1792], P(('dp', 'mp'))
All inputs are finite; a program needn't handle non-finite values.
Results may differ from a plain program's by a relative error of at most 0.0042.
Values may be sent and summed in bfloat16 or wider, within the bound.
A program may use at most 128 MiB of HBM per device.

v0:
```python
import jax
import jax.numpy as jnp
from jax import lax
from jax.sharding import PartitionSpec as P


def on_device(tokens, norm_gain, norm_bias, w_in, b_in, w_out, b_out):
    values = tokens.astype(jnp.float32)
    center = jnp.mean(values, axis=1, keepdims=True)
    spread = jnp.mean((values - center) ** 2, axis=1, keepdims=True)
    normed = ((values - center) / jnp.sqrt(spread + 1e-06) * norm_gain + norm_bias).astype(
        jnp.bfloat16
    )
    w_in_full = lax.all_gather(w_in, "dp", axis=0, tiled=True)
    gathered = lax.all_gather(normed, "mp", axis=0, tiled=True)
    pre = jnp.dot(gathered, w_in_full, preferred_element_type=jnp.float32) + b_in
    hidden = jax.nn.gelu(pre, approximate=False).astype(jnp.bfloat16)
    w_out_full = lax.all_gather(w_out, "dp", axis=1, tiled=True)
    summed = lax.psum_scatter(
        jnp.dot(hidden, w_out_full, preferred_element_type=jnp.float32),
        "mp",
        scatter_dimension=0,
        tiled=True,
    )
    return (values + summed + b_out).astype(jnp.bfloat16)


def solution(mesh):
    placed = (P(("dp", "mp"), None), P(), P(), P("dp", "mp"), P("mp"), P("mp", "dp"), P())
    return jax.shard_map(
        on_device, mesh=mesh, in_specs=placed, out_specs=P(("dp", "mp"), None), check_vma=False
    )
```

profile of v0, /device:TPU:0, one launch (start us, length us, event | category | flops | bytes accessed | tf_op | source)
XLA Modules:
  0.0 249.3 jit_solution(16586171305829466705)
XLA Ops:
  6.5 0.0 copy-start.2
  6.5 0.0 all-gather.4.cloned.1.call-start
  6.5 1.0 convert_reduce_fusion
  7.6 1.1 fusion.45
  8.7 1.7 fusion.48
  10.5 0.0 all-gather.4.cloned.1.call-update
  10.5 0.0 all-gather.6.cloned.1.call-start
  10.5 0.7 all-gather.6.cloned.1.call-update
  11.2 0.0 all-gather.8.cloned.1.call-start
  11.3 0.7 all-gather.8.cloned.1.call-update
  12.0 0.0 copy-start
  12.0 0.0 copy-start.1
  12.0 0.0 reduce-scatter.2.cloned.1.call-start
  12.0 42.5 %all-gather.4.cloned.1.call-done = bf16[320,1792]{1,0:T(8,128)(2,1)} async-done(((bf16[40,1792]{1,0:T(8,128)(2,1)}), bf16[320,1792]{1,0:T(8,128)(2,1)}) %all-gather.4.cloned.1.call-update) | async-done | bytes 1146896 | tf_op jit(solution)/shard_map/all_gather | solution.py:15
  54.6 49.7 %all-gather.6.cloned.1.call-done = bf16[1792,1920]{1,0:T(8,128)(2,1)} async-done(((bf16[448,1920]{1,0:T(8,128)(2,1)}), bf16[1792,1920]{1,0:T(8,128)(2,1)}) %all-gather.6.cloned.1.call-update) | async-done | bytes 6881296 | tf_op jit(solution)/shard_map/all_gather | solution.py:14
  104.3 51.3 %all-gather.8.cloned.1.call-done = bf16[1920,1792]{0,1:T(8,128)(2,1)} async-done(((bf16[1920,448]{0,1:T(8,128)(2,1)}), bf16[1920,1792]{0,1:T(8,128)(2,1)}) %all-gather.8.cloned.1.call-update) | async-done | bytes 6881296 | tf_op jit(solution)/shard_map/all_gather | solution.py:18
  155.6 0.0 copy-done.2
  155.6 15.7 %fusion.10 = f32[320,1792]{1,0:T(8,128)} fusion(bf16[1920,1792]{0,1:T(8,128)(2,1)} %all-gather.8.cloned.1.call-done, bf16[320,1792]{1,0:T(8,128)(2,1)} %all-gather.4.cloned.1.call-done, bf16[1792,1920]{1,0:T(8,128)(2,1)} %all-gather.6.cloned.1.call-done, f32[1920]{0:T(1024)S(1)} %copy-done.2), kind=kOutput, calls=%fused_computation.20 | convolution fusion | flops 4444569600 | bytes 17210880 | tf_op jit(solution)/shard_map/dot_general | solution.py:20
  171.3 0.0 reduce-scatter.2.cloned.1.call-update
  171.4 69.7 %reduce-scatter.2.cloned.1.call-done = f32[40,1792]{1,0:T(8,128)} async-done(((f32[320,1792]{1,0:T(8,128)}), f32[40,1792]{1,0:T(8,128)}) %reduce-scatter.2.cloned.1.call-update) | async-done | bytes 286736 | tf_op jit(solution)/shard_map/reduce_scatter | solution.py:19
  241.1 0.0 copy-done
  241.1 0.0 copy-done.1
  241.1 1.7 fusion.50
  (2 shorter events, 0.0 us)
Async XLA Ops:
  6.5 149.1 %copy-start.2 = (f32[1920]{0:T(1024)S(1)}, f32[1920]{0:T(1024)}, u32[]{:S(2)}) copy-start(f32[1920]{0:T(1024)} %param.11) | copy-start | bytes 23044
  6.5 48.0 %all-gather.4.cloned.1.call-start = ((), (), s32[]{:S(2)}) async-start(), calls=%async_computation.1 | async-start | bytes 1290240 | tf_op jit(solution)/shard_map/all_gather | solution.py:15
  10.5 93.8 %all-gather.6.cloned.1.call-start = ((), (), s32[]{:S(2)}) async-start(), calls=%async_computation.2 | async-start | bytes 8601600 | tf_op jit(solution)/shard_map/all_gather | solution.py:14
  11.2 144.4 %all-gather.8.cloned.1.call-start = ((), (), s32[]{:S(2)}) async-start(), calls=%async_computation.3 | async-start | bytes 8601600 | tf_op jit(solution)/shard_map/all_gather | solution.py:18
  12.0 229.1 %copy-start = (bf16[40,1792]{1,0:T(8,128)(2,1)S(1)}, bf16[40,1792]{1,0:T(8,128)(2,1)}, u32[]{:S(2)}) copy-start(bf16[40,1792]{1,0:T(8,128)(2,1)} %param.7) | copy-start | bytes 430084
  12.0 229.1 %copy-start.1 = (f32[1792]{0:T(1024)S(1)}, f32[1792]{0:T(1024)}, u32[]{:S(2)}) copy-start(f32[1792]{0:T(1024)} %param.13) | copy-start | bytes 21508
  12.0 229.1 %reduce-scatter.2.cloned.1.call-start = ((), (), s32[]{:S(2)}) async-start(), calls=%async_computation.4 | async-start | bytes 2580480 | tf_op jit(solution)/shard_map/reduce_scatter | solution.py:19
Sparse Core Ops, SparseCore 0:
  10.6 43.9 all-gather.3
  56.1 48.1 all-gather.5
  105.9 49.6 all-gather.7
  171.5 69.5 reduce-scatter.1
where the time goes:
time: 249 us
  waiting for transfers between devices  215 us (86%)
  matrix products  15.7 us (6%)
  between operations  13.2 us (5%)
  other arithmetic  5.56 us (2%)
    reduce_scatter x1, waiting for transfers between devices, on_device(): lax.psum_scatter(jnp.dot(hidden, w_out_full, preferred_element_type=jnp.f...  69.7 us
    all_gather x1, waiting for transfers between devices, on_device(): w_out_full = lax.all_gather(w_out, 'dp', axis=1, tiled=True)  51.3 us
    all_gather x1, waiting for transfers between devices, on_device(): w_in_full = lax.all_gather(w_in, 'dp', axis=0, tiled=True)  49.7 us
    all_gather x1, waiting for transfers between devices, on_device(): gathered = lax.all_gather(normed, 'mp', axis=0, tiled=True)  42.5 us
    dot_general x1, matrix products, on_device(): jnp.dot(hidden, w_out_full, preferred_element_type=jnp.float32)  15.7 us
  transfers between devices with their start and end apart: 4, of which 4 were waited for; matrix products, arithmetic and copies ran while one was open for 0% of the time, Pallas kernels for 0%

commit v1 on v0

--- a/solution.py
+++ b/solution.py
@@ -12,7 +12,12 @@
         jnp.bfloat16
     )
     w_in_full = lax.all_gather(w_in, "dp", axis=0, tiled=True)
-    gathered = lax.all_gather(normed, "mp", axis=0, tiled=True)
+    ring = [normed]
+    for hop in range(7):
+        ring.append(lax.ppermute(ring[-1], "mp", [(dev, (dev + 1) % 8) for dev in range(8)]))
+    gathered = jnp.roll(
+        jnp.concatenate(ring[::-1], axis=0), (lax.axis_index("mp") + 1) * ring[0].shape[0], axis=0
+    )
     pre = jnp.dot(gathered, w_in_full, preferred_element_type=jnp.float32) + b_in
     hidden = jax.nn.gelu(pre, approximate=False).astype(jnp.bfloat16)
     w_out_full = lax.all_gather(w_out, "dp", axis=1, tiled=True)

time: 249 us -> 206 us (0.83)
  waiting for transfers between devices: 215 us -> 172 us
  other arithmetic: 5.56 us -> 2.4 us
  starting transfers between devices: 0.12 us -> 3.14 us
    ppermute x0 -> x7, waiting for transfers between devices: none -> 54.8 us  [on_device(): lax.ppermute(ring[-1], 'mp', [(dev, (dev + 1) % 8) for dev in range(8)])]
    all_gather x1, waiting for transfers between devices: 49.7 us -> 0.02 us  [on_device(): w_in_full = lax.all_gather(w_in, 'dp', axis=0, tiled=True)]
    all_gather x1 -> x0, waiting for transfers between devices: 42.5 us -> none  [on_device(): gathered = lax.all_gather(normed, 'mp', axis=0, tiled=True)]
    all_gather x1, waiting for transfers between devices: 51.3 us -> 45.6 us  [on_device(): w_out_full = lax.all_gather(w_out, 'dp', axis=1, tiled=True)]
    ppermute x0 -> x7, starting transfers between devices: none -> 3.06 us  [on_device(): lax.ppermute(ring[-1], 'mp', [(dev, (dev + 1) % 8) for dev in range(8)])]
  transfers between devices with their start and end apart: 4 -> 10, of which waited for: 4 -> 9; matrix products, arithmetic and copies ran while one was open for 0% -> 0% of each run, Pallas kernels for 0% -> 0%
where the time goes in v1:
time: 206 us
  waiting for transfers between devices  172 us (83%)
  matrix products  15.4 us (7%)
  between operations  13.3 us (6%)
  starting transfers between devices  3.14 us (2%)
  other arithmetic  2.4 us (1%)
    reduce_scatter x1, waiting for transfers between devices, on_device(): lax.psum_scatter(jnp.dot(hidden, w_out_full, preferred_element_type=jnp.f...  69.8 us
    ppermute x7, waiting for transfers between devices, on_device(): lax.ppermute(ring[-1], 'mp', [(dev, (dev + 1) % 8) for dev in range(8)])  54.8 us
    all_gather x1, waiting for transfers between devices, on_device(): w_out_full = lax.all_gather(w_out, 'dp', axis=1, tiled=True)  45.6 us
    dot_general x1, matrix products, on_device(): jnp.dot(hidden, w_out_full, preferred_element_type=jnp.float32)  15.4 us
  transfers between devices with their start and end apart: 10, of which 9 were waited for; matrix products, arithmetic and copies ran while one was open for 0% of the time, Pallas kernels for 0%

profile of v1, /device:TPU:0, one launch (start us, length us, event | category | flops | bytes accessed | tf_op | source)
XLA Modules:
  0.0 206.1 jit_solution(7705632163236309295)
XLA Ops:
  6.5 0.7 all-gather.3.cloned.1.call-update
  7.3 0.0 all-gather.5.cloned.1.call-start
  7.3 0.7 all-gather.5.cloned.1.call-update
  8.0 0.0 reduce-scatter.2.cloned.1.call-start
  8.1 0.1 convert_reduce_fusion
  8.2 0.2 fusion.47
  8.4 0.0 copy-start.4
  8.5 0.1 fusion.50
  8.6 3.0 %collective-permute-start = (bf16[40,1792]{1,0:T(8,128)(2,1)S(1)}, bf16[40,1792]{1,0:T(8,128)(2,1)S(1)}, u32[]{:S(2)}, u32[]{:S(2)}) collective-permute-start(bf16[40,1792]{1,0:T(8,128)(2,1)S(1)} %fusion.50), channel_id=1, source_target_pairs={{0,1},{1,2},{2,3},{3,4},{4,5},{5,6},{6,7},{7,0},{8,9},{9,10},{10,1... | collective-permute-start | bytes 430088 | tf_op jit(solution)/shard_map/ppermute | solution.py:17
  11.6 6.8 %collective-permute-done = bf16[40,1792]{1,0:T(8,128)(2,1)S(1)} collective-permute-done((bf16[40,1792]{1,0:T(8,128)(2,1)S(1)}, bf16[40,1792]{1,0:T(8,128)(2,1)S(1)}, u32[]{:S(2)}, u32[]{:S(2)}) %collective-permute-start) | collective-permute-done | bytes 143392 | tf_op jit(solution)/shard_map/ppermute | solution.py:17
  18.4 7.8 %collective-permute-done.1 = bf16[40,1792]{1,0:T(8,128)(2,1)S(1)} collective-permute-done((bf16[40,1792]{1,0:T(8,128)(2,1)S(1)}, bf16[40,1792]{1,0:T(8,128)(2,1)S(1)}, u32[]{:S(2)}, u32[]{:S(2)}) %collective-permute-start.1) | collective-permute-done | bytes 143392 | tf_op jit(solution)/shard_map/ppermute | solution.py:17
  26.2 7.8 %collective-permute-done.2 = bf16[40,1792]{1,0:T(8,128)(2,1)S(1)} collective-permute-done((bf16[40,1792]{1,0:T(8,128)(2,1)S(1)}, bf16[40,1792]{1,0:T(8,128)(2,1)S(1)}, u32[]{:S(2)}, u32[]{:S(2)}) %collective-permute-start.2) | collective-permute-done | bytes 143392 | tf_op jit(solution)/shard_map/ppermute | solution.py:17
  34.0 7.8 %collective-permute-done.3 = bf16[40,1792]{1,0:T(8,128)(2,1)S(1)} collective-permute-done((bf16[40,1792]{1,0:T(8,128)(2,1)S(1)}, bf16[40,1792]{1,0:T(8,128)(2,1)S(1)}, u32[]{:S(2)}, u32[]{:S(2)}) %collective-permute-start.3) | collective-permute-done | bytes 143392 | tf_op jit(solution)/shard_map/ppermute | solution.py:17
  41.8 7.8 %collective-permute-done.4 = bf16[40,1792]{1,0:T(8,128)(2,1)S(1)} collective-permute-done((bf16[40,1792]{1,0:T(8,128)(2,1)S(1)}, bf16[40,1792]{1,0:T(8,128)(2,1)S(1)}, u32[]{:S(2)}, u32[]{:S(2)}) %collective-permute-start.4) | collective-permute-done | bytes 143392 | tf_op jit(solution)/shard_map/ppermute | solution.py:17
  49.7 9.0 %collective-permute-done.5 = bf16[40,1792]{1,0:T(8,128)(2,1)S(1)} collective-permute-done((bf16[40,1792]{1,0:T(8,128)(2,1)S(1)}, bf16[40,1792]{1,0:T(8,128)(2,1)S(1)}, u32[]{:S(2)}, u32[]{:S(2)}) %collective-permute-start.5) | collective-permute-done | bytes 143392 | tf_op jit(solution)/shard_map/ppermute | solution.py:17
  58.7 7.8 %collective-permute-done.6 = bf16[40,1792]{1,0:T(8,128)(2,1)S(1)} collective-permute-done((bf16[40,1792]{1,0:T(8,128)(2,1)S(1)}, bf16[40,1792]{1,0:T(8,128)(2,1)S(1)}, u32[]{:S(2)}, u32[]{:S(2)}) %collective-permute-start.6) | collective-permute-done | bytes 143392 | tf_op jit(solution)/shard_map/ppermute | solution.py:17
  66.6 0.1 constant_dynamic-update-slice_fusion.8
  66.9 0.1 constant_dynamic-update-slice_fusion
  67.0 0.0 all-gather.3.cloned.1.call-done
  67.0 45.6 %all-gather.5.cloned.1.call-done = bf16[1920,1792]{0,1:T(8,128)(2,1)} async-done(((bf16[1920,448]{0,1:T(8,128)(2,1)}), bf16[1920,1792]{0,1:T(8,128)(2,1)}) %all-gather.5.cloned.1.call-update) | async-done | bytes 6881296 | tf_op jit(solution)/shard_map/all_gather | solution.py:23
  112.7 15.4 %fusion.10 = f32[320,1792]{1,0:T(8,128)} fusion(bf16[1920,1792]{0,1:T(8,128)(2,1)} %all-gather.5.cloned.1.call-done, bf16[1792,1920]{1,0:T(8,128)(2,1)} %all-gather.3.cloned.1.call-done, f32[1920]{0:T(1024)S(1)} %copy-done.4, bf16[640,1792]{1,0:T(8,128)(2,1)S(1)} %constant_dynamic-update-slice_fusion, s32[]{:T(128)S(6)} %select_n.14), kind=kOutput, calls=%fused_computation.20 | convolution fusion | flops 4444569600 | bytes 17211396 | tf_op jit(solution)/shard_map/dot_general | solution.py:25
  128.1 0.0 reduce-scatter.2.cloned.1.call-update
  128.1 69.8 %reduce-scatter.2.cloned.1.call-done = f32[40,1792]{1,0:T(8,128)} async-done(((f32[320,1792]{1,0:T(8,128)}), f32[40,1792]{1,0:T(8,128)}) %reduce-scatter.2.cloned.1.call-update) | async-done | bytes 286736 | tf_op jit(solution)/shard_map/reduce_scatter | solution.py:24
  197.9 1.7 fusion.52
  (32 shorter events, 0.2 us)
Async XLA Ops:
  6.5 1.5 copy-start
  6.5 1.9 copy-start.2
  6.5 1.9 copy-start.1
  6.5 60.5 %all-gather.3.cloned.1.call-start = ((), (), s32[]{:S(2)}) async-start(), calls=%async_computation.1 | async-start | bytes 8601600 | tf_op jit(solution)/shard_map/all_gather | solution.py:14
  7.3 105.4 %all-gather.5.cloned.1.call-start = ((), (), s32[]{:S(2)}) async-start(), calls=%async_computation.2 | async-start | bytes 8601600 | tf_op jit(solution)/shard_map/all_gather | solution.py:23
  8.0 189.9 %reduce-scatter.2.cloned.1.call-start = ((), (), s32[]{:S(2)}) async-start(), calls=%async_computation.3 | async-start | bytes 2580480 | tf_op jit(solution)/shard_map/reduce_scatter | solution.py:24
  8.4 104.2 %copy-start.4 = (f32[1920]{0:T(1024)S(1)}, f32[1920]{0:T(1024)}, u32[]{:S(2)}) copy-start(f32[1920]{0:T(1024)} %param.11) | copy-start | bytes 23044
  8.6 9.8 %collective-permute-start = (bf16[40,1792]{1,0:T(8,128)(2,1)S(1)}, bf16[40,1792]{1,0:T(8,128)(2,1)S(1)}, u32[]{:S(2)}, u32[]{:S(2)}) collective-permute-start(bf16[40,1792]{1,0:T(8,128)(2,1)S(1)} %fusion.50), channel_id=1, source_target_pairs={{0,1},{1,2},{2,3},{3,4},{4,5},{5,6},{6,7},{7,0},{8,9},{9,10},{10,1... | collective-permute-start | bytes 430088 | tf_op jit(solution)/shard_map/ppermute | solution.py:17
  18.4 7.8 %collective-permute-start.1 = (bf16[40,1792]{1,0:T(8,128)(2,1)S(1)}, bf16[40,1792]{1,0:T(8,128)(2,1)S(1)}, u32[]{:S(2)}, u32[]{:S(2)}) collective-permute-start(bf16[40,1792]{1,0:T(8,128)(2,1)S(1)} %collective-permute-done), channel_id=1, source_target_pairs={{0,1},{1,2},{2,3},{3,4},{4,5},{5,6},{6,7},{7,0},{8,9},{9,10},{10,1... | collective-permute-start | bytes 430088 | tf_op jit(solution)/shard_map/ppermute | solution.py:17
  26.2 7.8 %collective-permute-start.2 = (bf16[40,1792]{1,0:T(8,128)(2,1)S(1)}, bf16[40,1792]{1,0:T(8,128)(2,1)S(1)}, u32[]{:S(2)}, u32[]{:S(2)}) collective-permute-start(bf16[40,1792]{1,0:T(8,128)(2,1)S(1)} %collective-permute-done.1), channel_id=1, source_target_pairs={{0,1},{1,2},{2,3},{3,4},{4,5},{5,6},{6,7},{7,0},{8,9},{9,10},{10,1... | collective-permute-start | bytes 430088 | tf_op jit(solution)/shard_map/ppermute | solution.py:17
  34.0 7.8 %collective-permute-start.3 = (bf16[40,1792]{1,0:T(8,128)(2,1)S(1)}, bf16[40,1792]{1,0:T(8,128)(2,1)S(1)}, u32[]{:S(2)}, u32[]{:S(2)}) collective-permute-start(bf16[40,1792]{1,0:T(8,128)(2,1)S(1)} %collective-permute-done.2), channel_id=1, source_target_pairs={{0,1},{1,2},{2,3},{3,4},{4,5},{5,6},{6,7},{7,0},{8,9},{9,10},{10,1... | collective-permute-start | bytes 430088 | tf_op jit(solution)/shard_map/ppermute | solution.py:17
  41.8 7.8 %collective-permute-start.4 = (bf16[40,1792]{1,0:T(8,128)(2,1)S(1)}, bf16[40,1792]{1,0:T(8,128)(2,1)S(1)}, u32[]{:S(2)}, u32[]{:S(2)}) collective-permute-start(bf16[40,1792]{1,0:T(8,128)(2,1)S(1)} %collective-permute-done.3), channel_id=1, source_target_pairs={{0,1},{1,2},{2,3},{3,4},{4,5},{5,6},{6,7},{7,0},{8,9},{9,10},{10,1... | collective-permute-start | bytes 430088 | tf_op jit(solution)/shard_map/ppermute | solution.py:17
  49.7 9.0 %collective-permute-start.5 = (bf16[40,1792]{1,0:T(8,128)(2,1)S(1)}, bf16[40,1792]{1,0:T(8,128)(2,1)S(1)}, u32[]{:S(2)}, u32[]{:S(2)}) collective-permute-start(bf16[40,1792]{1,0:T(8,128)(2,1)S(1)} %collective-permute-done.4), channel_id=1, source_target_pairs={{0,1},{1,2},{2,3},{3,4},{4,5},{5,6},{6,7},{7,0},{8,9},{9,10},{10,1... | collective-permute-start | bytes 430088 | tf_op jit(solution)/shard_map/ppermute | solution.py:17
  58.7 7.8 %collective-permute-start.6 = (bf16[40,1792]{1,0:T(8,128)(2,1)S(1)}, bf16[40,1792]{1,0:T(8,128)(2,1)S(1)}, u32[]{:S(2)}, u32[]{:S(2)}) collective-permute-start(bf16[40,1792]{1,0:T(8,128)(2,1)S(1)} %collective-permute-done.5), channel_id=1, source_target_pairs={{0,1},{1,2},{2,3},{3,4},{4,5},{5,6},{6,7},{7,0},{8,9},{9,10},{10,1... | collective-permute-start | bytes 430088 | tf_op jit(solution)/shard_map/ppermute | solution.py:17
  67.0 130.9 %copy-start.3 = (f32[1792]{0:T(1024)S(1)}, f32[1792]{0:T(1024)}, u32[]{:S(2)}) copy-start(f32[1792]{0:T(1024)} %param.13) | copy-start | bytes 21508
Sparse Core Ops, SparseCore 0:
  8.9 52.4 all-gather.2
  62.9 49.6 all-gather.4
  128.2 69.6 reduce-scatter.1
